TPU v7x, 32 devices: a whole 2x2x4 slice. The times are simulated.
32 devices in a mesh: groups: 2 (over y), cells: 8 (over z, x), side: 2 (over core).
Axes of the slice: x: 2, y: 2, z: 4, core: 2. Of those that a mesh axis runs over, the one named last changes fastest.
Arguments:
- datasets: float32 [2, 2000, 8192], P('side', None, ('groups', 'cells')), parts along dimension 2, may hold values from -6 to 6
- sketch: float32 [64, 8192], P(None, ('groups', 'cells')), parts along dimension 1, may hold values from -6 to 6
Outputs:
- factors: float32 [2, 64, 8192], P('side', None, ('groups', 'cells')), parts along dimension 2
There are 2 independent parts, one for each index of `groups`. A program takes and returns all parts, laid end to end along the dimension named above; each array names one. Nothing has to cross between parts.
All inputs are finite; a program needn't handle non-finite values.
Results may differ from a plain program's by a relative error of at most 0.00009.
Values sent between devices are 32-bit elements; how exact they have to be, the bound alone decides.
A program may use at most 64 MiB of HBM per device.

v0:
```python
import jax
import jax.numpy as jnp
from jax import lax
from jax.sharding import PartitionSpec as P


def from_behind(value, axis, steps):
    count = lax.axis_size(axis)
    initial, last = (max(0, -steps), min(count, count - steps))
    return lax.ppermute(value, axis, [(source, source + steps) for source in range(initial, last)])


def per_device(datasets, sketch):
    high = lax.Precision.HIGHEST
    own_data = datasets[0]
    side_index = lax.axis_index("side")
    cell_count = own_data.shape[1] * lax.axis_size("cells")
    scale = jnp.sqrt(jnp.float32(cell_count))
    partial_value = jnp.dot(sketch, own_data.T, precision=high)
    summed = lax.psum(partial_value, "cells")
    arrived = from_behind(summed, "side", -1)
    panel = jnp.where(side_index == 0, arrived, summed)
    range_rows = jnp.dot(panel, own_data, precision=high)
    gram_part = jnp.dot(range_rows, range_rows.T, precision=high)
    raw_part = jnp.dot(range_rows, own_data.T, precision=high)
    gram, raw_cross = lax.psum((gram_part, raw_part), "cells")
    lower = jnp.linalg.cholesky(gram)
    basis = jax.scipy.linalg.solve_triangular(lower, range_rows, lower=True)
    cross = jax.scipy.linalg.solve_triangular(lower, raw_cross, lower=True)
    received = from_behind(cross, "side", 1)
    projected = jnp.dot(received, own_data, precision=high)
    result = jnp.where(side_index == 0, basis * scale, projected / scale)
    return result[None]


def solution(mesh):
    in_specs = (P("side", None, ("groups", "cells")), P(None, ("groups", "cells")))
    out_specs = P("side", None, ("groups", "cells"))
    return jax.shard_map(
        per_device, mesh=mesh, in_specs=in_specs, out_specs=out_specs, check_vma=False
    )
```

profile of v0, /device:TPU:0, one launch (start us, length us, event | category | flops | bytes accessed | tf_op | source)
XLA Modules:
  0.0 225.7 jit_solution(7290744189002880673)
XLA Ops:
  6.5 0.0 copy-start
  6.5 0.0 all-reduce.3.cloned.1.call-start
  6.5 0.9 copy-done
  7.4 6.7 %fusion.6 = f32[64,2000]{1,0:T(8,128)} fusion(f32[64,512]{1,0:T(8,128)S(1)} %copy-done, f32[1,2000,512]{2,1,0:T(8,128)} %param.2), kind=kOutput, calls=%fused_computation.6 | convolution fusion | flops 786432000 | bytes 4739072 | tf_op jit(solution)/shard_map/dot_general | solution.py:19
  14.1 0.0 all-reduce.3.cloned.1.call-update
  14.2 0.0 all-reduce.5.cloned.1.call-start
  14.2 75.5 %all-reduce.3.cloned.1.call-done = f32[64,2000]{1,0:T(8,128)} async-done(((f32[64,2000]{1,0:T(8,128)}), f32[64,2000]{1,0:T(8,128)}) %all-reduce.3.cloned.1.call-update) | async-done | bytes 512016 | tf_op jit(solution)/shard_map/psum | solution.py:20
  89.7 1.3 collective-permute-start
  91.0 0.0 copy-start.1
  91.0 2.7 %collective-permute-done = f32[64,2000]{1,0:T(8,128)S(1)} collective-permute-done((f32[64,2000]{1,0:T(8,128)}, f32[64,2000]{1,0:T(8,128)S(1)}, u32[]{:S(2)}, u32[]{:S(2)}) %collective-permute-start) | collective-permute-done | bytes 512032 | tf_op jit(solution)/shard_map/ppermute | solution.py:10
  93.7 4.8 %fusion.4 = f32[64,512]{1,0:T(8,128)S(1)} fusion(f32[1,2000,512]{2,1,0:T(8,128)} %param.2, f32[64,2000]{1,0:T(8,128)S(1)} %collective-permute-done, f32[64,2000]{1,0:T(8,128)} %all-reduce.3.cloned.1.call-done, pred[]{:T(512)S(6)} %eq.4), kind=kOutput, calls=%fused_computation.4 | convolution fusion | flops 786560000 | bytes 5251073 | tf_op jit(solution)/shard_map/dot_general | solution.py:23
  98.5 0.3 fusion.24
  98.7 0.0 copy-done.1
  98.7 4.6 %fusion.2 = f32[64,2000]{1,0:T(8,128)} fusion(f32[64,512]{1,0:T(8,128)S(1)} %fusion.4, f32[1,2000,512]{2,1,0:T(8,128)S(1)} %copy-done.1), kind=kOutput, calls=%fused_computation.2 | convolution fusion | flops 786432000 | bytes 4739072 | tf_op jit(solution)/shard_map/dot_general | solution.py:25
  103.3 35.4 %psum.22 = f32[64,64]{0,1:T(8,128)S(1)} all-reduce(f32[64,64]{0,1:T(8,128)S(1)} %fusion.24), channel_id=1, replica_groups=mesh['groups'=2,'cells'=8,'side'=2] {'cells'}, use_global_device_ids=true, to_apply=%region_1.2 | all-reduce | flops 4096 | bytes 32768 | tf_op jit(solution)/shard_map/psum | solution.py:26
  138.7 0.1 copy.4
  138.8 0.0 all-reduce.5.cloned.1.call-update
  138.8 5.8 %cholesky.16 = f32[64,64]{1,0:T(8,128)S(1)} custom-call(f32[64,64]{1,0:T(8,128)S(1)} %fusion.23), custom_call_target="Cholesky" | custom-call | tf_op jit(solution)/shard_map/jit(cholesky)/cholesky | solution.py:27
  144.7 0.6 compare_reduce_fusion
  145.3 0.7 fusion.19
  146.0 4.9 %custom-call.10 = f32[1,64,64]{1,2,0:T(8,128)S(1)} custom-call(f32[1,64,64]{2,1,0:T(8,128)S(1)} %fusion.19), custom_call_target="InvertDiagBlocksLowerTriangular" | custom-call | tf_op jit(solution)/shard_map/jit(_solve_triangular)/triangular_solve | solution.py:28
  150.9 58.1 %all-reduce.5.cloned.1.call-done = f32[64,2000]{1,0:T(8,128)} async-done(((f32[64,2000]{1,0:T(8,128)}), f32[64,2000]{1,0:T(8,128)}) %all-reduce.5.cloned.1.call-update) | async-done | bytes 512016 | tf_op jit(solution)/shard_map/psum | solution.py:26
  209.0 1.7 fusion.20
  210.6 1.3 collective-permute-start.1
  212.0 0.3 convolution_multiply_fusion
  212.3 1.2 collective-permute-done.1
  213.5 5.4 %fusion.14 = f32[1,64,512]{2,1,0:T(8,128)} fusion(f32[64,512]{1,0:T(8,128)S(1)} %convolution_multiply_fusion, f32[64,2000]{1,0:T(8,128)S(1)} %collective-permute-done.1, f32[1,2000,512]{2,1,0:T(8,128)} %param.2, pred[]{:T(512)S(6)} %eq.4), kind=kOutput, calls=%fused_computation.10 | convolution fusion | flops 786497536 | bytes 4870145 | tf_op jit(solution)/shard_map/dot_general | solution.py:31
  (2 shorter events, 0.0 us)
Async XLA Ops:
  6.5 0.9 copy-start
  6.5 83.2 %all-reduce.3.cloned.1.call-start = ((), (), s32[]{:S(2)}) async-start(), calls=%async_computation | async-start | bytes 1048576 | tf_op jit(solution)/shard_map/psum | solution.py:20
  14.2 194.8 %all-reduce.5.cloned.1.call-start = ((), (), s32[]{:S(2)}) async-start(), calls=%async_computation.1 | async-start | bytes 1048576 | tf_op jit(solution)/shard_map/psum | solution.py:26
  89.7 4.0 %collective-permute-start = (f32[64,2000]{1,0:T(8,128)}, f32[64,2000]{1,0:T(8,128)S(1)}, u32[]{:S(2)}, u32[]{:S(2)}) collective-permute-start(f32[64,2000]{1,0:T(8,128)} %all-reduce.3.cloned.1.call-done), channel_id=1, source_target_pairs={{1,0},{3,2},{5,4},{7,6},{9,8},{11,10},{13,12},{15,14},{17,16},{19,... | collective-permute-start | bytes 1536008 | tf_op jit(solution)/shard_map/ppermute | solution.py:10
  91.0 7.7 %copy-start.1 = (f32[1,2000,512]{2,1,0:T(8,128)S(1)}, f32[1,2000,512]{2,1,0:T(8,128)}, u32[]{:S(2)}) copy-start(f32[1,2000,512]{2,1,0:T(8,128)} %param.2) | copy-start | bytes 12288004
  210.6 2.8 %collective-permute-start.1 = (f32[64,2000]{1,0:T(8,128)S(1)}, f32[64,2000]{1,0:T(8,128)S(1)}, u32[]{:S(2)}, u32[]{:S(2)}) collective-permute-start(f32[64,2000]{1,0:T(8,128)S(1)} %fusion.20), channel_id=1, source_target_pairs={{0,1},{2,3},{4,5},{6,7},{8,9},{10,11},{12,13},{14,15},{16,17},{18,... | collective-permute-start | bytes 1536008 | tf_op jit(solution)/shard_map/ppermute | solution.py:10
Sparse Core Ops, SparseCore 0:
  14.3 75.3 all-reduce.2
  138.9 70.0 all-reduce.4
where the time goes:
time: 226 us
  waiting for transfers between devices  137 us (61%)
  blocking collectives  35.4 us (16%)
  matrix products  23.7 us (10%)
  between operations  13.5 us (6%)
  other arithmetic  12.1 us (5%)
  starting transfers between devices  2.65 us (1%)
    psum x1, waiting for transfers between devices, per_device(): summed = lax.psum(partial_value, 'cells')  75.5 us
    psum x1, waiting for transfers between devices, per_device(): gram, raw_cross = lax.psum((gram_part, raw_part), 'cells')  58.1 us
    psum x1, blocking collectives, per_device(): gram, raw_cross = lax.psum((gram_part, raw_part), 'cells')  35.4 us
    dot_general x1, matrix products, per_device(): partial_value = jnp.dot(sketch, own_data.T, precision=high)  6.69 us
    another operation x3, other arithmetic, per_device(): lower = jnp.linalg.cholesky(gram)  6.52 us
    another operation x2, other arithmetic, per_device(): basis = jax.scipy.linalg.solve_triangular(lower, range_rows, lower=True)  5.55 us
    dot_general x1, matrix products, per_device(): projected = jnp.dot(received, own_data, precision=high)  5.43 us
    dot_general x1, matrix products, per_device(): range_rows = jnp.dot(panel, own_data, precision=high)  4.75 us
  transfers between devices with their start and end apart: 4, of which 4 were waited for; matrix products, arithmetic and copies ran while one was open for 5% of the time, Pallas kernels for 0%

commit v1 on v0

--- a/solution.py
+++ b/solution.py
@@ -2,6 +2,11 @@
 import jax.numpy as jnp
 from jax import lax
 from jax.sharding import PartitionSpec as P
+
+
+def gather_and_add(x, name):
+    shards = lax.all_gather(x, name)
+    return jnp.sum(shards, axis=0)
 
 
 def from_behind(value, axis, steps):
@@ -17,7 +22,7 @@
     cell_count = own_data.shape[1] * lax.axis_size("cells")
     scale = jnp.sqrt(jnp.float32(cell_count))
     partial_value = jnp.dot(sketch, own_data.T, precision=high)
-    summed = lax.psum(partial_value, "cells")
+    summed = gather_and_add(partial_value, "cells")
     arrived = from_behind(summed, "side", -1)
     panel = jnp.where(side_index == 0, arrived, summed)
     range_rows = jnp.dot(panel, own_data, precision=high)

time: 226 us -> 228 us (level)
  other arithmetic: 12.1 us -> 14.6 us
    all_gather x0 -> x1, waiting for transfers between devices: none -> 75.6 us  [gather_and_add(): shards = lax.all_gather(x, name)]
    psum x1 -> x0, waiting for transfers between devices: 75.5 us -> none  [per_device(): summed = lax.psum(partial_value, 'cells')]
    reduce_sum x0 -> x1, other arithmetic: none -> 2.5 us  [gather_and_add(): return jnp.sum(shards, axis=0)]
where the time goes in v1:
time: 228 us
  waiting for transfers between devices  137 us (60%)
  blocking collectives  34.7 us (15%)
  matrix products  23.7 us (10%)
  other arithmetic  14.6 us (6%)
  between operations  13.5 us (6%)
  starting transfers between devices  2.84 us (1%)
    all_gather x1, waiting for transfers between devices, gather_and_add(): shards = lax.all_gather(x, name)  75.6 us
    psum x1, waiting for transfers between devices, per_device(): gram, raw_cross = lax.psum((gram_part, raw_part), 'cells')  58 us
    psum x1, blocking collectives, per_device(): gram, raw_cross = lax.psum((gram_part, raw_part), 'cells')  34.7 us
    dot_general x1, matrix products, per_device(): partial_value = jnp.dot(sketch, own_data.T, precision=high)  6.67 us
    another operation x3, other arithmetic, per_device(): lower = jnp.linalg.cholesky(gram)  6.52 us
    another operation x2, other arithmetic, per_device(): basis = jax.scipy.linalg.solve_triangular(lower, range_rows, lower=True)  5.55 us
    dot_general x1, matrix products, per_device(): projected = jnp.dot(received, own_data, precision=high)  5.42 us
    dot_general x1, matrix products, per_device(): range_rows = jnp.dot(panel, own_data, precision=high)  4.75 us
  transfers between devices with their start and end apart: 4, of which 4 were waited for; matrix products, arithmetic and copies ran while one was open for 5% of the time, Pallas kernels for 0%

profile of v1, /device:TPU:0, one launch (start us, length us, event | category | flops | bytes accessed | tf_op | source)
XLA Modules:
  0.0 227.6 jit_solution(13135063198504549264)
XLA Ops:
  6.5 0.0 copy-start
  6.5 0.0 all-gather.3.cloned.1.call-start
  6.5 0.9 copy-done
  7.4 6.7 %fusion.6 = f32[64,2000]{1,0:T(8,128)} fusion(f32[64,512]{1,0:T(8,128)S(1)} %copy-done, f32[1,2000,512]{2,1,0:T(8,128)} %param.2), kind=kOutput, calls=%fused_computation.6 | convolution fusion | flops 786432000 | bytes 4739072 | tf_op jit(solution)/shard_map/dot_general | solution.py:24
  14.1 0.0 all-gather.3.cloned.1.call-update
  14.1 0.0 all-reduce.2.cloned.1.call-start
  14.2 75.6 %all-gather.3.cloned.1.call-done = f32[512,2000]{1,0:T(8,128)} async-done(((f32[64,2000]{1,0:T(8,128)}), f32[512,2000]{1,0:T(8,128)}) %all-gather.3.cloned.1.call-update) | async-done | bytes 4096016 | tf_op jit(solution)/shard_map/all_gather | solution.py:8
  89.8 2.5 %reduce_sum.9 = f32[64,2000]{1,0:T(8,128)S(1)} reduce(f32[8,64,2000]{2,1,0:T(8,128)} %bitcast.36, f32[]{:T(128)} %constant.54.clone.1), dimensions={0}, to_apply=%region_0.0 | reduce | flops 896000 | bytes 4608004 | tf_op jit(solution)/shard_map/reduce_sum | solution.py:9
  92.3 1.3 collective-permute-start
  93.6 0.0 copy-start.1
  93.6 2.5 %collective-permute-done = f32[64,2000]{1,0:T(8,128)S(1)} collective-permute-done((f32[64,2000]{1,0:T(8,128)S(1)}, f32[64,2000]{1,0:T(8,128)S(1)}, u32[]{:S(2)}, u32[]{:S(2)}) %collective-permute-start) | collective-permute-done | bytes 512032 | tf_op jit(solution)/shard_map/ppermute | solution.py:15
  96.1 4.7 %fusion.4 = f32[64,512]{1,0:T(8,128)S(1)} fusion(f32[1,2000,512]{2,1,0:T(8,128)} %param.2, f32[64,2000]{1,0:T(8,128)S(1)} %collective-permute-done, f32[64,2000]{1,0:T(8,128)S(1)} %reduce_sum.9, pred[]{:T(512)S(6)} %eq.4), kind=kOutput, calls=%fused_computation.4 | convolution fusion | flops 786560000 | bytes 5251073 | tf_op jit(solution)/shard_map/dot_general | solution.py:28
  100.9 0.3 fusion.24
  101.1 0.0 copy-done.1
  101.2 4.6 %fusion.2 = f32[64,2000]{1,0:T(8,128)} fusion(f32[64,512]{1,0:T(8,128)S(1)} %fusion.4, f32[1,2000,512]{2,1,0:T(8,128)S(1)} %copy-done.1), kind=kOutput, calls=%fused_computation.2 | convolution fusion | flops 786432000 | bytes 4739072 | tf_op jit(solution)/shard_map/dot_general | solution.py:30
  105.7 34.7 %psum.14 = f32[64,64]{0,1:T(8,128)S(1)} all-reduce(f32[64,64]{0,1:T(8,128)S(1)} %fusion.24), channel_id=1, replica_groups=mesh['groups'=2,'cells'=8,'side'=2] {'cells'}, use_global_device_ids=true, to_apply=%region_1.2 | all-reduce | flops 4096 | bytes 32768 | tf_op jit(solution)/shard_map/psum | solution.py:31
  140.4 0.1 copy.4
  140.5 0.0 all-reduce.2.cloned.1.call-update
  140.6 5.8 %cholesky.16 = f32[64,64]{1,0:T(8,128)S(1)} custom-call(f32[64,64]{1,0:T(8,128)S(1)} %fusion.23), custom_call_target="Cholesky" | custom-call | tf_op jit(solution)/shard_map/jit(cholesky)/cholesky | solution.py:32
  146.4 0.6 compare_reduce_fusion
  147.1 0.7 fusion.19
  147.7 4.9 %custom-call.10 = f32[1,64,64]{1,2,0:T(8,128)S(1)} custom-call(f32[1,64,64]{2,1,0:T(8,128)S(1)} %fusion.19), custom_call_target="InvertDiagBlocksLowerTriangular" | custom-call | tf_op jit(solution)/shard_map/jit(_solve_triangular)/triangular_solve | solution.py:33
  152.6 58.0 %all-reduce.2.cloned.1.call-done = f32[64,2000]{1,0:T(8,128)} async-done(((f32[64,2000]{1,0:T(8,128)}), f32[64,2000]{1,0:T(8,128)}) %all-reduce.2.cloned.1.call-update) | async-done | bytes 512016 | tf_op jit(solution)/shard_map/psum | solution.py:31
  210.7 1.7 fusion.20
  212.3 1.5 collective-permute-start.1
  213.8 0.3 convolution_multiply_fusion
  214.2 1.2 collective-permute-done.1
  215.3 5.4 %fusion.14 = f32[1,64,512]{2,1,0:T(8,128)} fusion(f32[64,512]{1,0:T(8,128)S(1)} %convolution_multiply_fusion, f32[64,2000]{1,0:T(8,128)S(1)} %collective-permute-done.1, f32[1,2000,512]{2,1,0:T(8,128)} %param.2, pred[]{:T(512)S(6)} %eq.4), kind=kOutput, calls=%fused_computation.10 | convolution fusion | flops 786497536 | bytes 4870145 | tf_op jit(solution)/shard_map/dot_general | solution.py:36
  (2 shorter events, 0.0 us)
Async XLA Ops:
  6.5 0.9 copy-start
  6.5 83.3 %all-gather.3.cloned.1.call-start = ((), (), s32[]{:S(2)}) async-start(), calls=%async_computation.1 | async-start | bytes 4718592 | tf_op jit(solution)/shard_map/all_gather | solution.py:8
  14.1 196.5 %all-reduce.2.cloned.1.call-start = ((), (), s32[]{:S(2)}) async-start(), calls=%async_computation | async-start | bytes 1048576 | tf_op jit(solution)/shard_map/psum | solution.py:31
  92.3 3.8 %collective-permute-start = (f32[64,2000]{1,0:T(8,128)S(1)}, f32[64,2000]{1,0:T(8,128)S(1)}, u32[]{:S(2)}, u32[]{:S(2)}) collective-permute-start(f32[64,2000]{1,0:T(8,128)S(1)} %reduce_sum.9), channel_id=1, source_target_pairs={{1,0},{3,2},{5,4},{7,6},{9,8},{11,10},{13,12},{15,14},{17,16},{19,... | collective-permute-start | bytes 1536008 | tf_op jit(solution)/shard_map/ppermute | solution.py:15
  93.6 7.5 %copy-start.1 = (f32[1,2000,512]{2,1,0:T(8,128)S(1)}, f32[1,2000,512]{2,1,0:T(8,128)}, u32[]{:S(2)}) copy-start(f32[1,2000,512]{2,1,0:T(8,128)} %param.2) | copy-start | bytes 12288004
  212.3 3.0 %collective-permute-start.1 = (f32[64,2000]{1,0:T(8,128)S(1)}, f32[64,2000]{1,0:T(8,128)S(1)}, u32[]{:S(2)}, u32[]{:S(2)}) collective-permute-start(f32[64,2000]{1,0:T(8,128)S(1)} %fusion.20), channel_id=1, source_target_pairs={{0,1},{2,3},{4,5},{6,7},{8,9},{10,11},{12,13},{14,15},{16,17},{18,... | collective-permute-start | bytes 1536008 | tf_op jit(solution)/shard_map/ppermute | solution.py:15
Sparse Core Ops, SparseCore 0:
  14.3 75.5 all-gather.2
  140.7 69.9 all-reduce.1
